TPU v7x, 32 devices: a whole 2x2x4 slice. The times are simulated.
32 devices in a mesh: dp: 8 (over y, x, core), seq: 4 (over z).
Axes of the slice: x: 2, y: 2, z: 4, core: 2. Of those that a mesh axis runs over, the one named last changes fastest.
Arguments:
- hidden_in: bfloat16 [8, 512, 2048], P('dp', 'seq'), may hold values from -6 to 6
- cotangent: bfloat16 [8, 512, 2048], P('dp', 'seq'), may hold values from -6 to 6
- norm_gain: float32 [2048], P('dp'), may hold values from 0.1 to 1.9
- route_weights: float32 [8, 512, 10], P('dp', 'seq'), may hold values from 0.1 to 1
- expert_ids: int32 [8, 512, 10], P('dp', 'seq'), may hold values from 0 to 63, all different within a row; in each aligned block of 128 rows (0 to 127, 128 to 255, ..., all dimensions but the last counted through in order) at most 24 rows name the same one
- expert_gate: bfloat16 [64, 2048, 512], P(('dp', 'seq')), may hold values from -0.125 to 0.125
- expert_up: bfloat16 [64, 2048, 512], P(('dp', 'seq')), may hold values from -0.125 to 0.125
- expert_down: bfloat16 [64, 512, 2048], P(('dp', 'seq')), may hold values from -0.25 to 0.25
Outputs:
- grad_hidden: bfloat16 [8, 512, 2048], P('dp', 'seq')
- grad_gain: float32 [2048], P('dp')
- grad_gate: bfloat16 [64, 2048, 512], P(('dp', 'seq'))
- grad_up: bfloat16 [64, 2048, 512], P(('dp', 'seq'))
- grad_down: bfloat16 [64, 512, 2048], P(('dp', 'seq'))
Inputs may be any that keep to these rules, and one draw needn't show every extreme that they name: `expert_ids`: each token names 10 different experts. Among the rows of one device no expert is named by more than 24 of them, and in some device one expert is named by exactly 24.
All inputs are finite; a program needn't handle non-finite values.
Results may differ from a plain program's by a relative error of at most 0.0072.
Values may be sent and summed in bfloat16 or wider, within the bound.
No kernel may reach another device: no remote copies, remote signals or barrier semaphores. Data moves between devices by JAX's collectives and lax.ppermute only.
A program may use at most 192 MiB of HBM per device.

v0:
```python
import jax
import jax.numpy as jnp
from jax import lax
from jax.sharding import PartitionSpec as P

TOP = 10


EPSILON = 1e-06


def shards(
    hidden_in, cotangent, norm_gain, route_weights, expert_ids, expert_gate, expert_up, expert_down
):
    tokens_here = hidden_in.shape[1]
    model_width = hidden_in.shape[2]
    local_experts = expert_gate.shape[0]
    dp_count = lax.axis_size("dp")
    seq_count = lax.axis_size("seq")
    devices = dp_count * seq_count
    expert_count = local_experts * devices
    capacity = max(2, tokens_here * TOP * 6 // (5 * expert_count))
    assignments = tokens_here * TOP
    gain_full = lax.all_gather(norm_gain, "dp", axis=0, tiled=True)
    inputs = hidden_in[0].astype(jnp.float32)
    inverse_root = lax.rsqrt(jnp.mean(inputs * inputs, axis=1, keepdims=True) + EPSILON)
    scaled = inputs * inverse_root
    normed = (scaled * gain_full[None, :]).astype(jnp.bfloat16)
    upstream = cotangent[0]
    weighted = (route_weights[0][:, :, None] * upstream[:, None, :].astype(jnp.float32)).astype(
        jnp.bfloat16
    )
    weighted = weighted.reshape(assignments, model_width)
    flat_experts = expert_ids[0].reshape(assignments)
    onehot = (flat_experts[:, None] == jnp.arange(expert_count, dtype=jnp.int32)[None, :]).astype(
        jnp.bfloat16
    )
    position = jnp.arange(assignments, dtype=jnp.int32)
    earlier = (position[:, None] > position[None, :]).astype(jnp.bfloat16)
    before = jnp.dot(earlier, onehot, preferred_element_type=jnp.float32)
    earlier_count = jnp.sum(before * onehot.astype(jnp.float32), axis=1).astype(jnp.int32)
    slot_index = flat_experts * capacity + earlier_count
    slot_entry = jnp.zeros((expert_count * capacity,), jnp.int32).at[slot_index].set(position + 1)
    occupied = slot_entry > 0
    source = jnp.maximum(slot_entry - 1, 0)
    zero_value = jnp.zeros((), jnp.bfloat16)
    flat_shape = (devices, local_experts * capacity, model_width)
    send_rows = jnp.where(occupied[:, None], normed[source // TOP], zero_value).reshape(flat_shape)
    send_grads = jnp.where(occupied[:, None], weighted[source], zero_value).reshape(flat_shape)
    arrived_rows, arrived_grads = (
        lax.all_to_all(send_rows, ("dp", "seq"), split_axis=0, concat_axis=0, tiled=True),
        lax.all_to_all(send_grads, ("dp", "seq"), split_axis=0, concat_axis=0, tiled=True),
    )
    four_shape = (devices, local_experts, capacity, model_width)
    rows_in = arrived_rows.reshape(four_shape)
    rows_grad = arrived_grads.reshape(four_shape)
    pre_gate = jnp.einsum(
        "nicd,idf->nicf", rows_in, expert_gate, preferred_element_type=jnp.float32
    )
    pre_up = jnp.einsum("nicd,idf->nicf", rows_in, expert_up, preferred_element_type=jnp.float32)
    sigmoid_gate = jax.nn.sigmoid(pre_gate)
    silu_gate = pre_gate * sigmoid_gate
    activation = (silu_gate * pre_up).astype(jnp.bfloat16)
    grad_act = jnp.einsum(
        "nicd,ifd->nicf", rows_grad, expert_down, preferred_element_type=jnp.float32
    )
    gate_back = (grad_act * pre_up * sigmoid_gate * (1.0 + pre_gate * (1.0 - sigmoid_gate))).astype(
        jnp.bfloat16
    )
    up_back = (grad_act * silu_gate).astype(jnp.bfloat16)
    grad_down = jnp.einsum(
        "nicf,nicd->ifd", activation, rows_grad, preferred_element_type=jnp.float32
    ).astype(jnp.bfloat16)
    grad_gate = jnp.einsum(
        "nicd,nicf->idf", rows_in, gate_back, preferred_element_type=jnp.float32
    ).astype(jnp.bfloat16)
    grad_up = jnp.einsum(
        "nicd,nicf->idf", rows_in, up_back, preferred_element_type=jnp.float32
    ).astype(jnp.bfloat16)
    returned = (
        jnp.einsum("nicf,idf->nicd", gate_back, expert_gate, preferred_element_type=jnp.float32)
        + jnp.einsum("nicf,idf->nicd", up_back, expert_up, preferred_element_type=jnp.float32)
    ).astype(jnp.bfloat16)
    back_rows = lax.all_to_all(
        returned.reshape(flat_shape), ("dp", "seq"), split_axis=0, concat_axis=0, tiled=True
    )
    back_flat = back_rows.reshape(expert_count * capacity, model_width)
    summed = jnp.sum(
        back_flat[slot_index].astype(jnp.float32).reshape(tokens_here, TOP, model_width), axis=1
    )
    local_gain = jnp.sum(summed * scaled, axis=0)
    partial_share = lax.psum_scatter(local_gain, "dp", scatter_dimension=0, tiled=True)
    grad_gain = lax.psum(partial_share, "seq")
    gained = summed * gain_full[None, :]
    centered = jnp.mean(gained * scaled, axis=1, keepdims=True)
    grad_hidden = (
        upstream.astype(jnp.float32) + inverse_root * (gained - scaled * centered)
    ).astype(jnp.bfloat16)
    return (grad_hidden.reshape(hidden_in.shape), grad_gain, grad_gate, grad_up, grad_down)


def solution(mesh):
    return jax.shard_map(
        shards,
        mesh=mesh,
        in_specs=(
            P("dp", "seq", None),
            P("dp", "seq", None),
            P("dp"),
            P("dp", "seq", None),
            P("dp", "seq", None),
            P(("dp", "seq"), None, None),
            P(("dp", "seq"), None, None),
            P(("dp", "seq"), None, None),
        ),
        out_specs=(
            P("dp", "seq", None),
            P("dp"),
            P(("dp", "seq"), None, None),
            P(("dp", "seq"), None, None),
            P(("dp", "seq"), None, None),
        ),
        check_vma=False,
    )
```

profile of v0, /device:TPU:0, one launch (start us, length us, event | category | flops | bytes accessed | tf_op | source)
XLA Modules:
  0.0 598.8 jit_solution(17626287329584033442)
XLA Ops:
  0.7 0.0 copy-start.4
  0.7 0.8 broadcast_multiply_fusion
  1.5 0.8 copy.33
  2.3 0.1 copy.32
  2.4 0.1 mul.125
  2.5 0.1 eq.15
  2.6 0.8 fusion.36
  3.5 5.2 scatter_custom_fusion
  8.8 0.2 fusion.41
  9.0 10.4 %all-gather = f32[8,1,256]{2,1,0:T(1,128)S(1)} all-gather(f32[1,1,256]{2,1,0:T(1,128)S(1)} %bitcast.124), channel_id=1, replica_groups=mesh['dp'=8,'seq'=4] {'dp'}, dimensions={0}, use_global_device_ids=true | all-gather | bytes 9216 | tf_op jit(solution)/shard_map/all_gather | solution.py:24
  19.5 0.1 copy.34
  19.6 0.1 mul.127
  19.7 0.1 broadcast_in_dim.35
  19.8 0.1 convert_bitcast_fusion.1
  19.9 7.9 %mul.129 = f32[128,10,2048]{2,1,0:T(8,128)} broadcast(f32[128,2048]{1,0:T(8,128)S(1)} %convert_bitcast_fusion.1), dimensions={0,2} | broadcast | bytes 11534336 | tf_op jit(solution)/shard_map/mul | solution.py:30
  27.9 13.9 %mul.130 = f32[1280,2048]{1,0:T(8,128)} reshape(f32[128,10,2048]{2,1,0:T(8,128)} %mul.129) | data formatting | bytes 20971520 | tf_op jit(solution)/shard_map/mul | solution.py:30
  41.8 0.2 fusion.38
  42.0 7.1 %gather_fusion.1 = bf16[1536,2048]{1,0:T(8,128)(2,1)} fusion(bf16[128,2048]{1,0:T(8,128)(2,1)S(1)} %fusion.38, s32[2048]{0:T(1024)S(1)} %pad_clamp_fusion.1), kind=kCustom, calls=%fused_computation.1 | custom fusion | bytes 12589056 | tf_op jit(solution)/shard_map/gather | solution.py:48
  49.1 7.0 %multiply_convert_fusion = bf16[1280,2048]{1,0:T(8,128)(2,1)} fusion(f32[1280,2048]{1,0:T(8,128)} %mul.130, f32[1280]{0:T(1024)S(1)} %mul.127), kind=kLoop, calls=%fused_computation.5 | loop fusion | flops 5242880 | bytes 15733760 | tf_op jit(solution)/shard_map/convert_element_type | solution.py:30
  56.1 15.9 %gather_fusion = bf16[1536,2048]{1,0:T(8,128)(2,1)} fusion(bf16[1280,2048]{1,0:T(8,128)(2,1)} %multiply_convert_fusion, s32[2048]{0:T(1024)S(1)} %pad_clamp_fusion.2), kind=kCustom, calls=%fused_computation | custom fusion | bytes 12589056 | tf_op jit(solution)/shard_map/gather | solution.py:49
  72.0 8.3 %broadcast_select_fusion.1 = (bf16[32,48,2048]{2,1,0:T(8,128)(2,1)}, bf16[32,48,2048]{2,1,0:T(8,128)(2,1)S(1)}) fusion(bf16[32,48,2048]{2,1,0:T(8,128)(2,1)} %bitcast.112, pred[32,48]{1,0:T(8,128)(4,1)S(1)} %broadcast_in_dim.35, bf16[32,48,2048]{2,1,0:T(8,128)(2,1)} %bitcast.111), kind=kLoop, calls=%fused_computation.13 | loop fusion | flops 6291456 | bytes 25167360 | tf_op jit(solution)/shard_map/jit(_where)/select_n | solution.py:49
  80.2 142.1 %all_to_all.15 = bf16[32,48,2048]{2,1,0:T(8,128)(2,1)} all-to-all(bf16[32,48,2048]{2,1,0:T(8,128)(2,1)S(1)} %get-tuple-element.12), channel_id=1, replica_groups=mesh['dp'=8,'seq'=4] {'dp','seq'}, dimensions={0} | all-to-all | bytes 12582912 | tf_op jit(solution)/shard_map/all_to_all | solution.py:51
  222.3 4.8 all-to-all-start
  227.2 9.3 %fusion.2 = f32[2,32,24,512]{3,2,1,0:T(8,128)} fusion(bf16[32,2,24,2048]{3,2,1,0:T(8,128)(2,1)} %bitcast.113, bf16[2,2048,512]{2,1,0:T(8,128)(2,1)} %param.13), kind=kOutput, calls=%fused_computation.14 | convolution fusion | flops 3221225472 | bytes 13631488 | tf_op jit(solution)/shard_map/nicd,idf->nicf/dot_general | solution.py:57
  236.4 5.2 fusion.4
  241.6 122.2 %all-to-all-done = bf16[32,48,2048]{2,1,0:T(8,128)(2,1)} async-done(((bf16[32,48,2048]{2,1,0:T(8,128)(2,1)}), bf16[32,48,2048]{2,1,0:T(8,128)(2,1)}, u32[]{:S(2)}, u32[]{:S(2)}) %all-to-all-start) | async-done | bytes 6291488 | tf_op jit(solution)/shard_map/all_to_all | solution.py:52
  363.8 10.4 %fusion.26 = (bf16[32,2,24,512]{3,2,0,1:T(8,128)(2,1)S(1)}, bf16[32,2,24,512]{3,2,0,1:T(8,128)(2,1)S(1)}) fusion(f32[2,32,24,512]{3,2,1,0:T(8,128)} %fusion.2, f32[2,32,24,512]{3,2,1,0:T(8,128)} %fusion.4, bf16[2,512,2048]{2,1,0:T(8,128)(2,1)} %param.15, bf16[32,2,24,2048]{3,2,1,0:T(8,128)(2,1)} %bitcast.3), kind=kOutput, calls=%fused_computation.42 | convolution fusion | flops 3231449088 | bytes 19922944 | tf_op jit(solution)/shard_map/nicd,ifd->nicf/dot_general | solution.py:64
  374.2 6.4 %fusion.10 = f32[2,32,24,2048]{3,2,1,0:T(8,128)} fusion(bf16[32,2,24,512]{3,2,0,1:T(8,128)(2,1)S(1)} %get-tuple-element.8, bf16[2,2048,512]{2,1,0:T(8,128)(2,1)S(1)} %copy-done.2), kind=kOutput, calls=%fused_computation.22 | convolution fusion | flops 3221225472 | bytes 18350080 | tf_op jit(solution)/shard_map/nicf,idf->nicd/dot_general | solution.py:81
  380.6 8.0 %fusion.1 = bf16[32,2,24,2048]{3,2,0,1:T(8,128)(2,1)S(1)} fusion(f32[2,32,24,2048]{3,2,1,0:T(8,128)} %fusion.10, bf16[32,2,24,512]{3,2,0,1:T(8,128)(2,1)S(1)} %get-tuple-element.7, bf16[2,2048,512]{2,1,0:T(8,128)(2,1)} %param.14), kind=kOutput, calls=%fused_computation.11 | convolution fusion | flops 3227516928 | bytes 24641536 | tf_op jit(solution)/shard_map/nicf,idf->nicd/dot_general | solution.py:82
  388.6 3.2 copy.38
  391.8 7.1 %all-to-all-start.2 = ((bf16[32,48,2048]{2,1,0:T(8,128)(2,1)}), bf16[32,48,2048]{2,1,0:T(8,128)(2,1)}, u32[]{:S(2)}, u32[]{:S(2)}) async-start(bf16[32,48,2048]{2,1,0:T(8,128)(2,1)} %bitcast.110), calls=%async_computation.2 | async-start | bytes 12582912 | tf_op jit(solution)/shard_map/all_to_all | solution.py:84
  398.9 0.6 dynamic-slice
  400.2 0.0 copy-start.7
  400.2 8.9 %bitcast_convert_fusion.1 = bf16[2,2048,512]{2,1,0:T(8,128)(2,1)} fusion(bf16[32,2,24,2048]{3,2,1,0:T(8,128)(2,1)} %bitcast.114, bf16[32,2,24,512]{3,2,0,1:T(8,128)(2,1)} %copy-done.8), kind=kOutput, calls=%fused_computation.7 | convolution fusion | flops 3223322624 | bytes 12058624 | tf_op jit(solution)/shard_map/nicd,nicf->idf/dot_general | solution.py:77
  409.1 0.0 copy-start.16
  409.1 5.1 bitcast_convert_fusion.2
  414.2 8.1 %bitcast_convert_fusion = bf16[2,512,2048]{2,1,0:T(8,128)(2,1)} fusion(bf16[32,2,24,2048]{3,2,1,0:T(8,128)(2,1)} %bitcast.3, f32[2,32,24,512]{3,2,1,0:T(8,128)S(1)} %copy-done.17, f32[2,32,24,512]{3,2,1,0:T(8,128)S(1)} %copy-done.16), kind=kOutput, calls=%fused_computation.6 | convolution fusion | flops 3228041216 | bytes 16777216 | tf_op jit(solution)/shard_map/nicf,nicd->ifd/dot_general | solution.py:71
  422.3 113.4 %all-to-all-done.2 = bf16[32,48,2048]{2,1,0:T(8,128)(2,1)} async-done(((bf16[32,48,2048]{2,1,0:T(8,128)(2,1)}), bf16[32,48,2048]{2,1,0:T(8,128)(2,1)}, u32[]{:S(2)}, u32[]{:S(2)}) %all-to-all-start.2) | async-done | bytes 6291488 | tf_op jit(solution)/shard_map/all_to_all | solution.py:84
  535.6 14.4 %gather_fusion.2 = bf16[1280,2048]{1,0:T(8,128)(2,1)} fusion(bf16[1536,2048]{1,0:T(8,128)(2,1)} %bitcast.20, s32[2048]{0:T(1024)S(1)} %pad_clamp_fusion), kind=kCustom, calls=%fused_computation.2 | custom fusion | bytes 10490880 | tf_op jit(solution)/shard_map/gather | solution.py:89
  550.0 10.6 %reshape.157 = f32[128,10,2048]{2,1,0:T(8,128)} reshape(bf16[1280,2048]{1,0:T(8,128)(2,1)} %gather_fusion.2) | data formatting | bytes 15728640 | tf_op jit(solution)/shard_map/convert_element_type | solution.py:89
  560.6 0.0 copy-start.10
  560.6 0.0 copy-start.13
  560.7 9.9 %reduce_sum.49 = f32[128,2048]{1,0:T(8,128)S(1)} reduce(f32[128,10,2048]{2,1,0:T(8,128)} %reshape.157, f32[]{:T(128)} %constant.12.clone.1), dimensions={1}, to_apply=%region_3.4 | reduce | flops 2359296 | bytes 11534340 | tf_op jit(solution)/shard_map/reduce_sum | solution.py:88
  570.6 0.4 fusion.40
  570.9 15.0 %all-reduce = f32[2048]{0:T(1024)S(1)} all-reduce(f32[2048]{0:T(1024)S(1)} %get-tuple-element.5), channel_id=2, replica_groups=mesh['dp'=8,'seq'=4] {'dp'}, use_global_device_ids=true, to_apply=%region_6.7.clone | all-reduce | flops 2048 | bytes 16384
  585.9 0.1 dynamic-slice.1
  586.0 11.1 %psum.7 = f32[256]{0:T(256)} all-reduce(f32[256]{0:T(256)S(1)} %dynamic-slice.1), channel_id=1, replica_groups=mesh['dp'=8,'seq'=4] {'seq'}, use_global_device_ids=true, to_apply=%region_7.8 | all-reduce | flops 256 | bytes 2048 | tf_op jit(solution)/shard_map/psum | solution.py:93
  597.1 1.2 fusion.37
  (51 shorter events, 0.2 us)
Async XLA Ops:
  0.6 8.2 %copy-start = (bf16[1,128,2048]{2,1,0:T(8,128)(2,1)S(1)}, bf16[1,128,2048]{2,1,0:T(8,128)(2,1)}, u32[]{:S(2)}) copy-start(bf16[1,128,2048]{2,1,0:T(8,128)(2,1)} %param.8) | copy-start | bytes 1572868
  0.6 8.4 %copy-start.14 = (f32[256]{0:T(256)S(1)}, f32[256]{0:T(256)}, u32[]{:S(2)}) copy-start(f32[256]{0:T(256)} %param.10) | copy-start | bytes 3076
  0.7 18.8 %copy-start.11 = (f32[1,128,10]{1,0,2:T(1,128)S(1)}, f32[1,128,10]{1,0,2:T(1,128)}, u32[]{:S(2)}) copy-start(f32[1,128,10]{1,0,2:T(1,128)} %param.11) | copy-start | bytes 15364
  0.7 19.2 %copy-start.4 = (bf16[1,128,2048]{2,1,0:T(8,128)(2,1)S(1)}, bf16[1,128,2048]{2,1,0:T(8,128)(2,1)}, u32[]{:S(2)}) copy-start(bf16[1,128,2048]{2,1,0:T(8,128)(2,1)} %param.9) | copy-start | bytes 1572868
  9.0 32.8 %copy-start.12 = (f32[128]{0:T(128)}, f32[128]{0:T(128)S(1)}, u32[]{:S(2)}) copy-start(f32[128]{0:T(128)S(1)} %add_rsqrt_fusion) | copy-start | bytes 1540
  19.5 22.3 %copy-start.9 = (f32[8,1,256]{2,1,0:T(1,128)}, f32[8,1,256]{2,1,0:T(1,128)S(1)}, u32[]{:S(2)}) copy-start(f32[8,1,256]{2,1,0:T(1,128)S(1)} %all-gather) | copy-start | bytes 24580
  222.3 14.1 %slice-start = ((s8[6291456]{0:T(1024)(128)(4,1)}), s8[2097152]{0:T(1024)(128)(4,1)S(1)}, s32[]{:S(2)}) async-start(s8[6291456]{0:T(1024)(128)(4,1)} %bitcast.115), calls=%async_computation.3 | async-start | bytes 4194304
  222.3 141.5 %all-to-all-start = ((bf16[32,48,2048]{2,1,0:T(8,128)(2,1)}), bf16[32,48,2048]{2,1,0:T(8,128)(2,1)}, u32[]{:S(2)}, u32[]{:S(2)}) async-start(bf16[32,48,2048]{2,1,0:T(8,128)(2,1)} %get-tuple-element.11), calls=%async_computation | async-start | bytes 12582912 | tf_op jit(solution)/shard_map/all_to_all | solution.py:52
  227.1 9.3 %slice-start.1 = ((s8[6291456]{0:T(1024)(128)(4,1)}), s8[4194304]{0:T(1024)(128)(4,1)S(1)}, s32[]{:S(2)}) async-start(s8[6291456]{0:T(1024)(128)(4,1)} %bitcast.115), calls=%async_computation.4 | async-start | bytes 8388608
  227.1 9.3 %copy-start.3 = (bf16[2,2048,512]{2,1,0:T(8,128)(2,1)S(1)}, bf16[2,2048,512]{2,1,0:T(8,128)(2,1)}, u32[]{:S(2)}) copy-start(bf16[2,2048,512]{2,1,0:T(8,128)(2,1)} %param.14) | copy-start | bytes 12582916
  363.8 10.4 %copy-start.2 = (bf16[2,2048,512]{2,1,0:T(8,128)(2,1)S(1)}, bf16[2,2048,512]{2,1,0:T(8,128)(2,1)}, u32[]{:S(2)}) copy-start(bf16[2,2048,512]{2,1,0:T(8,128)(2,1)} %param.13) | copy-start | bytes 12582916
  374.2 6.4 %copy-start.6 = (bf16[32,2,24,512]{3,2,0,1:T(8,128)(2,1)}, bf16[32,2,24,512]{3,2,0,1:T(8,128)(2,1)S(1)}, u32[]{:S(2)}) copy-start(bf16[32,2,24,512]{3,2,0,1:T(8,128)(2,1)S(1)} %get-tuple-element.8) | copy-start | bytes 4718596
  374.2 6.4 %copy-start.8 = (bf16[32,2,24,512]{3,2,0,1:T(8,128)(2,1)}, bf16[32,2,24,512]{3,2,0,1:T(8,128)(2,1)S(1)}, u32[]{:S(2)}) copy-start(bf16[32,2,24,512]{3,2,0,1:T(8,128)(2,1)S(1)} %get-tuple-element.7) | copy-start | bytes 4718596
  391.8 7.1 %copy-start.15 = (u32[32]{0:T(128)S(1)}, u32[32]{0:T(128)}, u32[]{:S(2)}) copy-start(u32[32]{0:T(128)} %constant.45) | copy-start | bytes 388
  391.8 17.2 %slice-start.2 = ((s8[6291456]{0:T(1024)(128)(4,1)}), s8[2097152]{0:T(1024)(128)(4,1)S(1)}, s32[]{:S(2)}) async-start(s8[6291456]{0:T(1024)(128)(4,1)} %bitcast.118), calls=%async_computation.5 | async-start | bytes 4194304
  391.8 143.8 %all-to-all-start.2 = ((bf16[32,48,2048]{2,1,0:T(8,128)(2,1)}), bf16[32,48,2048]{2,1,0:T(8,128)(2,1)}, u32[]{:S(2)}, u32[]{:S(2)}) async-start(bf16[32,48,2048]{2,1,0:T(8,128)(2,1)} %bitcast.110), calls=%async_computation.2 | async-start | bytes 12582912 | tf_op jit(solution)/shard_map/all_to_all | solution.py:84
  400.2 8.9 %slice-start.3 = ((s8[6291456]{0:T(1024)(128)(4,1)}), s8[4194304]{0:T(1024)(128)(4,1)S(1)}, s32[]{:S(2)}) async-start(s8[6291456]{0:T(1024)(128)(4,1)} %bitcast.118), calls=%async_computation.6 | async-start | bytes 8388608
  400.2 8.9 %copy-start.7 = (bf16[32,2,24,512]{3,2,0,1:T(8,128)(2,1)S(1)}, bf16[32,2,24,512]{3,2,0,1:T(8,128)(2,1)}, u32[]{:S(2)}) copy-start(bf16[32,2,24,512]{3,2,0,1:T(8,128)(2,1)} %copy-done.6) | copy-start | bytes 4718596
  409.1 5.1 copy-start.16
  409.1 5.1 copy-start.17
  560.6 9.9 %copy-start.1 = (bf16[1,128,2048]{2,1,0:T(8,128)(2,1)S(1)}, bf16[1,128,2048]{2,1,0:T(8,128)(2,1)}, u32[]{:S(2)}) copy-start(bf16[1,128,2048]{2,1,0:T(8,128)(2,1)} %param.8) | copy-start | bytes 1572868
  560.6 9.9 %copy-start.10 = (f32[8,1,256]{2,1,0:T(1,128)S(1)}, f32[8,1,256]{2,1,0:T(1,128)}, u32[]{:S(2)}) copy-start(f32[8,1,256]{2,1,0:T(1,128)} %copy-done.9) | copy-start | bytes 24580
  560.6 9.9 %copy-start.13 = (f32[128]{0:T(128)S(1)}, f32[128]{0:T(128)}, u32[]{:S(2)}) copy-start(f32[128]{0:T(128)} %copy-done.12) | copy-start | bytes 1540
  560.6 36.5 %copy-start.5 = (bf16[1,128,2048]{2,1,0:T(8,128)(2,1)S(1)}, bf16[1,128,2048]{2,1,0:T(8,128)(2,1)}, u32[]{:S(2)}) copy-start(bf16[1,128,2048]{2,1,0:T(8,128)(2,1)} %param.9) | copy-start | bytes 1572868
where the time goes:
time: 606 us; the launch traced here: 599 us
  waiting for transfers between devices  236 us (39%)
  blocking collectives  179 us (30%)
  local copies, waits for them, and re-layouts  80.5 us (13%)
  matrix products  62 us (10%)
  other arithmetic  28 us (5%)
  starting transfers between devices  11.9 us (2%)
    all_to_all x1, blocking collectives, shards(): lax.all_to_all(send_rows, ('dp', 'seq'), split_axis=0, concat_axis=0, til...  142 us
    all_to_all x1, waiting for transfers between devices, shards(): lax.all_to_all(send_grads, ('dp', 'seq'), split_axis=0, concat_axis=0, ti...  122 us
    all_to_all x1, waiting for transfers between devices, shards(): lax.all_to_all(returned.reshape(flat_shape), ('dp', 'seq'), split_axis=0,...  113 us
    mul x3, local copies, waits for them, and re-layouts, shards(): route_weights[0][:, :, None] * upstream[:, None, :].astype(jnp.float32)  22 us
    gather x1, local copies, waits for them, and re-layouts, shards(): weighted[source]  15.9 us
    unnamed x1, blocking collectives  15 us
    gather x1, local copies, waits for them, and re-layouts, shards(): back_flat[slot_index].astype(jnp.float32)  14.4 us
  transfers between devices with their start and end apart: 2, of which 2 were waited for; matrix products, arithmetic and copies ran while one was open for 6% of the time, Pallas kernels for 0%

commit v1 on v0

v1 whole, which is shorter than its diff:
```python
import jax
import jax.numpy as jnp
from jax import lax
from jax.sharding import PartitionSpec as P

TOP = 10


EPSILON = 1e-06

def shards(
    hidden_in, cotangent, norm_gain, route_weights, expert_ids, expert_gate, expert_up, expert_down
):
    tokens_here = hidden_in.shape[1]
    model_width = hidden_in.shape[2]
    local_experts = expert_gate.shape[0]
    dp_count = lax.axis_size("dp")
    seq_count = lax.axis_size("seq")
    devices = dp_count * seq_count
    expert_count = local_experts * devices
    capacity = max(2, tokens_here * TOP * 6 // (5 * expert_count))
    dp_at = lax.axis_index("dp")
    seq_at = lax.axis_index("seq")
    my_index = dp_at * seq_count + seq_at

    upstream = cotangent[0]
    all_grads = lax.all_gather(upstream, ("dp", "seq"), axis=0)

    gain_full = lax.all_gather(norm_gain, "dp", axis=0, tiled=True)
    inputs = hidden_in[0].astype(jnp.float32)
    inverse_root = lax.rsqrt(jnp.mean(inputs * inputs, axis=1, keepdims=True) + EPSILON)
    scaled = inputs * inverse_root
    normed = (scaled * gain_full[None, :]).astype(jnp.bfloat16)
    all_rows = lax.all_gather(normed, ("dp", "seq"), axis=0)

    ids_here = expert_ids[0]
    weights_here = route_weights[0]
    ids_all = lax.all_gather(ids_here.T, ("dp", "seq"), axis=0, tiled=False)
    weights_all = lax.all_gather(weights_here.T, ("dp", "seq"), axis=0, tiled=False)

    place = jnp.arange(tokens_here, dtype=jnp.int32)
    upper = (place[:, None] < place[None, :]).astype(jnp.bfloat16)
    slots = jnp.arange(capacity, dtype=jnp.int32)
    my_experts = my_index * local_experts + jnp.arange(local_experts, dtype=jnp.int32)

    named = ids_all[:, None, :, :] == my_experts[None, :, None, None]
    chosen = jnp.any(named, axis=2)
    weight = jnp.sum(jnp.where(named, weights_all[:, None, :, :], 0.0), axis=2)
    rank = jnp.einsum(
        "nit,tu->niu", chosen.astype(jnp.bfloat16), upper, preferred_element_type=jnp.float32
    ).astype(jnp.int32)
    picks = chosen[:, :, None, :] & (rank[:, :, None, :] == slots[None, None, :, None])
    row_weight = jnp.sum(jnp.where(picks, weight[:, :, None, :], 0.0), axis=3)
    picks = picks.reshape(devices, local_experts * capacity, tokens_here).astype(jnp.bfloat16)
    row_weight = row_weight.reshape(devices, local_experts * capacity, 1)

    def pick(table):
        return jnp.einsum("nst,ntd->nsd", picks, table, preferred_element_type=jnp.float32)

    four_shape = (devices, local_experts, capacity, model_width)
    rows_grad = (row_weight * pick(all_grads)).astype(jnp.bfloat16).reshape(four_shape)
    rows_in = pick(all_rows).astype(jnp.bfloat16).reshape(four_shape)

    grad_act = jnp.einsum(
        "nicd,ifd->nicf", rows_grad, expert_down, preferred_element_type=jnp.float32
    )
    pre_gate = jnp.einsum(
        "nicd,idf->nicf", rows_in, expert_gate, preferred_element_type=jnp.float32
    )
    pre_up = jnp.einsum("nicd,idf->nicf", rows_in, expert_up, preferred_element_type=jnp.float32)
    sigmoid_gate = jax.nn.sigmoid(pre_gate)
    silu_gate = pre_gate * sigmoid_gate
    activation = (silu_gate * pre_up).astype(jnp.bfloat16)
    gate_back = (grad_act * pre_up * sigmoid_gate * (1.0 + pre_gate * (1.0 - sigmoid_gate))).astype(
        jnp.bfloat16
    )
    up_back = (grad_act * silu_gate).astype(jnp.bfloat16)
    returned = (
        jnp.einsum("nicf,idf->nicd", gate_back, expert_gate, preferred_element_type=jnp.float32)
        + jnp.einsum("nicf,idf->nicd", up_back, expert_up, preferred_element_type=jnp.float32)
    ).astype(jnp.bfloat16)

    back_rows = lax.all_to_all(
        returned.reshape(devices, local_experts * capacity, model_width),
        ("dp", "seq"),
        split_axis=0,
        concat_axis=0,
        tiled=True,
    )

    grad_down = jnp.einsum(
        "nicf,nicd->ifd", activation, rows_grad, preferred_element_type=jnp.float32
    ).astype(jnp.bfloat16)
    grad_gate = jnp.einsum(
        "nicd,nicf->idf", rows_in, gate_back, preferred_element_type=jnp.float32
    ).astype(jnp.bfloat16)
    grad_up = jnp.einsum(
        "nicd,nicf->idf", rows_in, up_back, preferred_element_type=jnp.float32
    ).astype(jnp.bfloat16)

    experts_range = jnp.arange(expert_count, dtype=jnp.int32)
    chosen_here = jnp.any(
        ids_here[:, :, None] == experts_range[None, None, :], axis=1
    )
    rank_here = jnp.dot(
        upper.T, chosen_here.astype(jnp.bfloat16), preferred_element_type=jnp.float32
    ).astype(jnp.int32)
    sums = (
        chosen_here[:, :, None] & (rank_here[:, :, None] == slots[None, None, :])
    ).reshape(tokens_here, expert_count * capacity).astype(jnp.bfloat16)
    summed = jnp.dot(
        sums,
        back_rows.reshape(expert_count * capacity, model_width),
        preferred_element_type=jnp.float32,
    )
    local_gain = jnp.sum(summed * scaled, axis=0)
    total_gain = lax.psum(local_gain, ("dp", "seq"))
    shard_width = norm_gain.shape[0]
    grad_gain = lax.dynamic_slice(total_gain, (dp_at * shard_width,), (shard_width,))
    gained = summed * gain_full[None, :]
    centered = jnp.mean(gained * scaled, axis=1, keepdims=True)
    grad_hidden = (
        upstream.astype(jnp.float32) + inverse_root * (gained - scaled * centered)
    ).astype(jnp.bfloat16)
    return (grad_hidden.reshape(hidden_in.shape), grad_gain, grad_gate, grad_up, grad_down)


def solution(mesh):
    return jax.shard_map(
        shards,
        mesh=mesh,
        in_specs=(
            P("dp", "seq", None),
            P("dp", "seq", None),
            P("dp"),
            P("dp", "seq", None),
            P("dp", "seq", None),
            P(("dp", "seq"), None, None),
            P(("dp", "seq"), None, None),
            P(("dp", "seq"), None, None),
        ),
        out_specs=(
            P("dp", "seq", None),
            P("dp"),
            P(("dp", "seq"), None, None),
            P(("dp", "seq"), None, None),
            P(("dp", "seq"), None, None),
        ),
        check_vma=False,
    )
```

time: 606 us -> 492 us (0.81); the launches traced: 599 us -> 492 us
  local copies, waits for them, and re-layouts: 80.5 us -> 6.33 us
  waiting for transfers between devices: 236 us -> 182 us
  other arithmetic: 28 us -> 5.47 us
  matrix products: 62 us -> 82.5 us
  blocking collectives: 179 us -> 197 us
  between operations: 2.12 us -> 14.3 us
  starting transfers between devices: 11.9 us -> 3.82 us
    all_gather x0 -> x2, blocking collectives: none -> 143 us  [the longest x1 74 us: shards(): lax.all_gather(weights_here.T, ('dp', 'seq'), axis=0, tiled=False)]
    all_to_all x1 -> x0, blocking collectives: 142 us -> none  [shards(): lax.all_to_all(send_rows, ('dp', 'seq'), split_axis=0, concat_axis=0, til...]
    all_to_all x2 -> x1, waiting for transfers between devices: 236 us -> 113 us  [shards(): lax.all_to_all(returned.reshape(devices, local_experts * capacity, model_...]
    all_gather x0 -> x2, waiting for transfers between devices: none -> 68.5 us  [the longest x1 68.5 us: shards(): all_grads = lax.all_gather(upstream, ('dp', 'seq'), axis=0)]
    gather x3 -> x0, local copies, waits for them, and re-layouts: 37.4 us -> none  [the longest x1 15.9 us: shards(): weighted[source]]
    psum x1, blocking collectives: 11.1 us -> 43.5 us  [shards(): total_gain = lax.psum(local_gain, ('dp', 'seq'))]
    mul x5 -> x1, local copies, waits for them, and re-layouts: 22.2 us -> 0.08 us  [shards(): row_weight * pick(all_grads)]
    dot_general x1 -> x5, matrix products: 0.82 us -> 21.1 us  [the longest x2 16.8 us: pick(): jnp.einsum('nst,ntd->nsd', picks, table, preferred_element_type=jnp.float32)]
  transfers between devices with their start and end apart: 2 -> 3, of which waited for: 2 -> 2; matrix products, arithmetic and copies ran while one was open for 6% -> 9% of each run, Pallas kernels for 0% -> 0%
where the time goes in v1:
time: 492 us
  blocking collectives  197 us (40%)
  waiting for transfers between devices  182 us (37%)
  matrix products  82.5 us (17%)
  between operations  14.3 us (3%)
  local copies, waits for them, and re-layouts  6.33 us (1%)
  other arithmetic  5.47 us (1%)
    all_to_all x1, waiting for transfers between devices, shards(): lax.all_to_all(returned.reshape(devices, local_experts * capacity, model_...  113 us
    all_gather x1, blocking collectives, shards(): lax.all_gather(weights_here.T, ('dp', 'seq'), axis=0, tiled=False)  74 us
    all_gather x1, blocking collectives, shards(): ids_all = lax.all_gather(ids_here.T, ('dp', 'seq'), axis=0, tiled=False)  69.5 us
    all_gather x1, waiting for transfers between devices, shards(): all_grads = lax.all_gather(upstream, ('dp', 'seq'), axis=0)  68.5 us
    psum x1, blocking collectives, shards(): total_gain = lax.psum(local_gain, ('dp', 'seq'))  43.5 us
    dot_general x2, matrix products, pick(): jnp.einsum('nst,ntd->nsd', picks, table, preferred_element_type=jnp.float32)  16.8 us
    all_gather x1, blocking collectives, shards(): gain_full = lax.all_gather(norm_gain, 'dp', axis=0, tiled=True)  10.6 us
    dot_general x1, matrix products, shards(): jnp.einsum('nicd,ifd->nicf', rows_grad, expert_down, preferred_element_ty...  9.94 us
  transfers between devices with their start and end apart: 3, of which 2 were waited for; matrix products, arithmetic and copies ran while one was open for 9% of the time, Pallas kernels for 0%

profile of v1, /device:TPU:0, one launch (start us, length us, event | category | flops | bytes accessed | tf_op | source)
XLA Modules:
  0.0 491.8 jit_solution(4126240018301125779)
XLA Ops:
  7.2 0.0 all-gather.10.cloned.1.call-start
  7.2 1.2 fusion.40
  8.5 10.6 %all-gather.4 = f32[8,1,256]{2,1,0:T(1,128)S(1)} all-gather(f32[1,1,256]{2,1,0:T(1,128)} %bitcast.164), channel_id=1, replica_groups=mesh['dp'=8,'seq'=4] {'dp'}, dimensions={0}, use_global_device_ids=true | all-gather | bytes 9216 | tf_op jit(solution)/shard_map/all_gather | solution.py:29
  19.0 0.6 copy-done.9
  19.6 2.0 fusion.42
  21.6 0.0 all-gather.10.cloned.1.call-update
  21.7 0.0 all-gather.8.cloned.1.call-start
  21.7 0.7 all-gather.8.cloned.1.call-update
  22.4 0.1 eq.88
  22.5 0.7 copy.91
  23.2 0.7 copy.92
  23.9 74.0 %all-gather.3 = f32[32,10,128]{2,1,0:T(8,128)S(1)} all-gather(f32[1,10,128]{2,1,0:T(8,128)S(1)} %bitcast.163), channel_id=3, replica_groups=mesh['dp'=8,'seq'=4] {'dp','seq'}, dimensions={0}, use_global_device_ids=true | all-gather | bytes 168960 | tf_op jit(solution)/shard_map/all_gather | solution.py:39
  97.8 0.1 copy.55
  97.9 69.5 %all-gather.2 = s32[32,10,128]{2,1,0:T(8,128)S(1)} all-gather(s32[1,10,128]{2,1,0:T(8,128)S(1)} %bitcast.161), channel_id=2, replica_groups=mesh['dp'=8,'seq'=4] {'dp','seq'}, dimensions={0}, use_global_device_ids=true | all-gather | bytes 168960 | tf_op jit(solution)/shard_map/all_gather | solution.py:38
  167.4 0.1 copy.52
  167.5 0.1 fusion.47
  167.6 0.1 compare_reduce_fusion
  167.7 0.1 convolution_convert_fusion.1
  167.9 0.4 select_reduce_fusion
  168.3 0.1 copy.57
  168.4 0.1 copy.58
  168.4 0.2 fusion.45
  168.7 0.0 all-gather.10.cloned.1.call-done
  168.7 0.0 copy-start.3
  168.7 8.7 %convolution_convert_fusion = bf16[32,48,2048]{2,1,0:T(8,128)(2,1)S(1)} fusion(pred[32,48,128]{2,1,0:T(8,128)(4,1)S(1)} %fusion.45, bf16[32,128,2048]{2,1,0:T(8,128)(2,1)} %all-gather.10.cloned.1.call-done), kind=kOutput, calls=%fused_computation.14 | convolution fusion | flops 808452096 | bytes 23265280 | tf_op jit(solution)/shard_map/nst,ntd->nsd/dot_general | solution.py:58
  177.4 0.0 copy-start.4
  177.4 5.1 %fusion.1 = f32[2,32,24,512]{3,2,1,0:T(8,128)} fusion(bf16[32,2,24,2048]{3,2,1,0:T(8,128)(2,1)S(1)} %bitcast.152, bf16[2,2048,512]{2,1,0:T(8,128)(2,1)S(1)} %copy-done.3), kind=kOutput, calls=%fused_computation.6 | convolution fusion | flops 3221225472 | bytes 13631488 | tf_op jit(solution)/shard_map/nicd,idf->nicf/dot_general | solution.py:67
  182.6 5.1 %fusion.3 = f32[2,32,24,512]{3,2,1,0:T(8,128)} fusion(bf16[32,2,24,2048]{3,2,1,0:T(8,128)(2,1)S(1)} %bitcast.153, bf16[2,2048,512]{2,1,0:T(8,128)(2,1)S(1)} %copy-done.4), kind=kOutput, calls=%fused_computation.8 | convolution fusion | flops 3221225472 | bytes 13631488 | tf_op jit(solution)/shard_map/nicd,idf->nicf/dot_general | solution.py:70
  187.7 68.5 %all-gather.8.cloned.1.call-done = bf16[32,128,2048]{2,1,0:T(8,128)(2,1)} async-done(((bf16[1,128,2048]{2,1,0:T(8,128)(2,1)}), bf16[32,128,2048]{2,1,0:T(8,128)(2,1)}) %all-gather.8.cloned.1.call-update) | async-done | bytes 16777232 | tf_op jit(solution)/shard_map/all_gather | solution.py:27
  256.2 8.1 %multiply_convert_fusion = bf16[32,48,2048]{2,1,0:T(8,128)(2,1)S(1)} fusion(f32[32,48]{1,0:T(8,128)S(1)} %copy.58, pred[32,48,128]{2,1,0:T(8,128)(4,1)S(1)} %fusion.45, bf16[32,128,2048]{2,1,0:T(8,128)(2,1)} %all-gather.8.cloned.1.call-done), kind=kOutput, calls=%fused_computation.1 | convolution fusion | flops 811597824 | bytes 23271424 | tf_op jit(solution)/shard_map/nst,ntd->nsd/dot_general | solution.py:58
  264.3 9.9 %fusion.25 = (bf16[32,2,24,512]{3,2,0,1:T(8,128)(2,1)S(1)}, bf16[32,2,24,512]{3,2,0,1:T(8,128)(2,1)S(1)}) fusion(f32[2,32,24,512]{3,2,1,0:T(8,128)} %fusion.1, f32[2,32,24,512]{3,2,1,0:T(8,128)} %fusion.3, bf16[2,512,2048]{2,1,0:T(8,128)(2,1)} %param.15, bf16[32,2,24,2048]{3,2,1,0:T(8,128)(2,1)S(1)} %bitcast.148), kind=kOutput, calls=%fused_computation.35 | convolution fusion | flops 3231449088 | bytes 19922944 | tf_op jit(solution)/shard_map/nicd,ifd->nicf/dot_general | solution.py:64
  274.2 0.0 copy-start.6
  274.3 9.8 %fusion.9 = f32[2,32,24,2048]{3,2,1,0:T(8,128)} fusion(bf16[32,2,24,512]{3,2,0,1:T(8,128)(2,1)S(1)} %get-tuple-element.8, bf16[2,2048,512]{2,1,0:T(8,128)(2,1)} %param.13), kind=kOutput, calls=%fused_computation.15 | convolution fusion | flops 3221225472 | bytes 18350080 | tf_op jit(solution)/shard_map/nicf,idf->nicd/dot_general | solution.py:79
  284.0 7.7 %fusion = bf16[32,2,24,2048]{3,2,0,1:T(8,128)(2,1)S(1)} fusion(f32[2,32,24,2048]{3,2,1,0:T(8,128)} %fusion.9, bf16[32,2,24,512]{3,2,0,1:T(8,128)(2,1)S(1)} %get-tuple-element.7, bf16[2,2048,512]{2,1,0:T(8,128)(2,1)} %param.14), kind=kOutput, calls=%fused_computation.5 | convolution fusion | flops 3227516928 | bytes 24641536 | tf_op jit(solution)/shard_map/nicf,idf->nicd/dot_general | solution.py:80
  291.8 3.2 copy.62
  295.0 3.7 all-to-all-start
  298.8 0.1 convolution_convert_fusion.2
  299.0 0.2 fusion.43
  299.1 0.0 copy-start.7
  299.2 8.9 %bitcast_convert_fusion.1 = bf16[2,2048,512]{2,1,0:T(8,128)(2,1)} fusion(bf16[32,2,24,2048]{3,2,1,0:T(8,128)(2,1)} %bitcast.154, bf16[32,2,24,512]{3,2,0,1:T(8,128)(2,1)} %copy-done.8), kind=kOutput, calls=%fused_computation.3 | convolution fusion | flops 3223322624 | bytes 12058624 | tf_op jit(solution)/shard_map/nicd,nicf->idf/dot_general | solution.py:97
  308.0 9.4 %bitcast_convert_fusion.2 = bf16[2,2048,512]{2,1,0:T(8,128)(2,1)} fusion(bf16[32,2,24,2048]{3,2,1,0:T(8,128)(2,1)} %bitcast.155, bf16[32,2,24,512]{3,2,0,1:T(8,128)(2,1)S(1)} %copy-done.7), kind=kOutput, calls=%fused_computation.4 | convolution fusion | flops 3223322624 | bytes 12058624 | tf_op jit(solution)/shard_map/nicd,nicf->idf/dot_general | solution.py:94
  317.5 5.4 %bitcast_convert_fusion = bf16[2,512,2048]{2,1,0:T(8,128)(2,1)} fusion(bf16[32,2,24,2048]{3,2,1,0:T(8,128)(2,1)S(1)} %bitcast.151, f32[2,32,24,512]{3,2,1,0:T(8,128)S(1)} %copy-done.14, f32[2,32,24,512]{3,2,1,0:T(8,128)S(1)} %copy-done.13), kind=kOutput, calls=%fused_computation.2 | convolution fusion | flops 3228041216 | bytes 16777216 | tf_op jit(solution)/shard_map/nicf,nicd->ifd/dot_general | solution.py:91
  322.9 112.6 %all-to-all-done = bf16[32,48,2048]{2,1,0:T(8,128)(2,1)} async-done(((bf16[32,48,2048]{2,1,0:T(8,128)(2,1)}), bf16[32,48,2048]{2,1,0:T(8,128)(2,1)}, u32[]{:S(2)}, u32[]{:S(2)}) %all-to-all-start) | async-done | bytes 6291488 | tf_op jit(solution)/shard_map/all_to_all | solution.py:83
  435.5 0.0 copy-start.5
  435.5 4.1 fusion.39
  439.6 43.5 %psum.7 = f32[2048]{0:T(1024)S(1)} all-reduce(f32[2048]{0:T(1024)S(1)} %get-tuple-element.5), channel_id=1, replica_groups=mesh['dp'=8,'seq'=4] {'dp','seq'}, use_global_device_ids=true, to_apply=%region_7.8 | all-reduce | flops 2048 | bytes 16384 | tf_op jit(solution)/shard_map/psum | solution.py:117
  483.1 0.6 dynamic_slice.3
  483.7 1.2 fusion.46
  (37 shorter events, 0.2 us)
Async XLA Ops:
  7.2 161.5 %all-gather.10.cloned.1.call-start = ((), (), s32[]{:S(2)}) async-start(), calls=%async_computation.2 | async-start | bytes 17301504 | tf_op jit(solution)/shard_map/all_gather | solution.py:34
  8.4 10.6 %copy-start.11 = (f32[128]{0:T(128)}, f32[128]{0:T(128)S(1)}, u32[]{:S(2)}) copy-start(f32[128]{0:T(128)S(1)} %add_rsqrt_fusion) | copy-start | bytes 1540
  19.0 0.6 copy-start.9
  21.7 234.5 %all-gather.8.cloned.1.call-start = ((), (), s32[]{:S(2)}) async-start(), calls=%async_computation.1 | async-start | bytes 17301504 | tf_op jit(solution)/shard_map/all_gather | solution.py:27
  168.7 8.7 %copy-start.3 = (bf16[2,2048,512]{2,1,0:T(8,128)(2,1)S(1)}, bf16[2,2048,512]{2,1,0:T(8,128)(2,1)}, u32[]{:S(2)}) copy-start(bf16[2,2048,512]{2,1,0:T(8,128)(2,1)} %param.13) | copy-start | bytes 12582916
  177.4 5.2 %copy-start.1 = (bf16[32,48,2048]{2,1,0:T(8,128)(2,1)}, bf16[32,48,2048]{2,1,0:T(8,128)(2,1)S(1)}, u32[]{:S(2)}) copy-start(bf16[32,48,2048]{2,1,0:T(8,128)(2,1)S(1)} %convolution_convert_fusion) | copy-start | bytes 18874372
  177.4 5.1 %copy-start.4 = (bf16[2,2048,512]{2,1,0:T(8,128)(2,1)S(1)}, bf16[2,2048,512]{2,1,0:T(8,128)(2,1)}, u32[]{:S(2)}) copy-start(bf16[2,2048,512]{2,1,0:T(8,128)(2,1)} %param.14) | copy-start | bytes 12582916
  264.3 10.0 %copy-start = (bf16[32,48,2048]{2,1,0:T(8,128)(2,1)}, bf16[32,48,2048]{2,1,0:T(8,128)(2,1)S(1)}, u32[]{:S(2)}) copy-start(bf16[32,48,2048]{2,1,0:T(8,128)(2,1)S(1)} %multiply_convert_fusion) | copy-start | bytes 18874372
  274.2 9.8 %copy-start.6 = (bf16[32,2,24,512]{3,2,0,1:T(8,128)(2,1)}, bf16[32,2,24,512]{3,2,0,1:T(8,128)(2,1)S(1)}, u32[]{:S(2)}) copy-start(bf16[32,2,24,512]{3,2,0,1:T(8,128)(2,1)S(1)} %get-tuple-element.8) | copy-start | bytes 4718596
  274.2 9.8 %copy-start.8 = (bf16[32,2,24,512]{3,2,0,1:T(8,128)(2,1)}, bf16[32,2,24,512]{3,2,0,1:T(8,128)(2,1)S(1)}, u32[]{:S(2)}) copy-start(bf16[32,2,24,512]{3,2,0,1:T(8,128)(2,1)S(1)} %get-tuple-element.7) | copy-start | bytes 4718596
  295.0 22.4 %slice-start = ((s8[6291456]{0:T(1024)(128)(4,1)}), s8[2097152]{0:T(1024)(128)(4,1)S(1)}, s32[]{:S(2)}) async-start(s8[6291456]{0:T(1024)(128)(4,1)} %bitcast.149), calls=%async_computation.3 | async-start | bytes 4194304
  295.0 140.5 %all-to-all-start = ((bf16[32,48,2048]{2,1,0:T(8,128)(2,1)}), bf16[32,48,2048]{2,1,0:T(8,128)(2,1)}, u32[]{:S(2)}, u32[]{:S(2)}) async-start(bf16[32,48,2048]{2,1,0:T(8,128)(2,1)} %bitcast.147), calls=%async_computation | async-start | bytes 12582912 | tf_op jit(solution)/shard_map/all_to_all | solution.py:83
  299.1 8.9 %copy-start.7 = (bf16[32,2,24,512]{3,2,0,1:T(8,128)(2,1)S(1)}, bf16[32,2,24,512]{3,2,0,1:T(8,128)(2,1)}, u32[]{:S(2)}) copy-start(bf16[32,2,24,512]{3,2,0,1:T(8,128)(2,1)} %copy-done.6) | copy-start | bytes 4718596
  299.2 18.3 %slice-start.1 = ((s8[6291456]{0:T(1024)(128)(4,1)}), s8[4194304]{0:T(1024)(128)(4,1)S(1)}, s32[]{:S(2)}) async-start(s8[6291456]{0:T(1024)(128)(4,1)} %bitcast.149), calls=%async_computation.4 | async-start | bytes 8388608
  308.0 9.4 %copy-start.13 = (f32[2,32,24,512]{3,2,1,0:T(8,128)S(1)}, f32[2,32,24,512]{3,2,1,0:T(8,128)}, u32[]{:S(2)}) copy-start(f32[2,32,24,512]{3,2,1,0:T(8,128)} %fusion.1) | copy-start | bytes 9437188
  308.0 9.4 %copy-start.14 = (f32[2,32,24,512]{3,2,1,0:T(8,128)S(1)}, f32[2,32,24,512]{3,2,1,0:T(8,128)}, u32[]{:S(2)}) copy-start(f32[2,32,24,512]{3,2,1,0:T(8,128)} %fusion.3) | copy-start | bytes 9437188
  317.5 118.0 %copy-start.2 = (bf16[1,128,2048]{2,1,0:T(8,128)(2,1)S(1)}, bf16[1,128,2048]{2,1,0:T(8,128)(2,1)}, u32[]{:S(2)}) copy-start(bf16[1,128,2048]{2,1,0:T(8,128)(2,1)} %param.8) | copy-start | bytes 1572868
  317.5 118.0 %copy-start.10 = (f32[8,1,256]{2,1,0:T(1,128)S(1)}, f32[8,1,256]{2,1,0:T(1,128)}, u32[]{:S(2)}) copy-start(f32[8,1,256]{2,1,0:T(1,128)} %copy-done.9) | copy-start | bytes 24580
  317.5 118.0 %copy-start.12 = (f32[128]{0:T(128)S(1)}, f32[128]{0:T(128)}, u32[]{:S(2)}) copy-start(f32[128]{0:T(128)} %copy-done.11) | copy-start | bytes 1540
  435.5 48.2 %copy-start.5 = (bf16[1,128,2048]{2,1,0:T(8,128)(2,1)S(1)}, bf16[1,128,2048]{2,1,0:T(8,128)(2,1)}, u32[]{:S(2)}) copy-start(bf16[1,128,2048]{2,1,0:T(8,128)(2,1)} %param.9) | copy-start | bytes 1572868
Sparse Core Ops, SparseCore 0:
  21.8 117.1 all-gather.9
  142.0 114.1 all-gather.7
